TPU v7x, 32 devices: a whole 2x2x4 slice. The times are simulated.
32 devices in a mesh: leaf: 8 (over z, y), grid: 4 (over x, core).
Axes of the slice: x: 2, y: 2, z: 4, core: 2. Of those that a mesh axis runs over, the one named last changes fastest.
Arguments:
- source_leaf: float32 [8, 4096], P(None, ('leaf', 'grid')), may hold values from -6 to 6
- block_leaf: float32 [4096, 128], P(('leaf', 'grid')), may hold values from -0.5 to 0.5
- expand_leaf: float32 [4096, 128], P(('leaf', 'grid')), may hold values from -0.5 to 0.5
- basis_leaf: float32 [4096, 256], P(('leaf', 'grid')), may hold values from -0.25 to 0.25
- pivot_leaf: float32 [4096], P(('leaf', 'grid')), may hold values from -2 to 2
- couple_leaf: float32 [8192, 128], P(('leaf', 'grid')), may hold values from -0.5 to 0.5
- ranks_leaf: int32 [8, 2], replicated, may hold values from 32 to 128
- targets_leaf: int32 [8192], P(('leaf', 'grid')), may hold values from 0 to 2047, as said below
- source_middle: float32 [8, 4096], P(None, ('leaf', 'grid')), may hold values from -6 to 6
- block_middle: float32 [4096, 128], P(('leaf', 'grid')), may hold values from -0.5 to 0.5
- expand_middle: float32 [4096, 128], P(('leaf', 'grid')), may hold values from -0.5 to 0.5
- basis_middle: float32 [4096, 256], P(('leaf', 'grid')), may hold values from -0.1875 to 0.1875
- pivot_middle: float32 [4096], P(('leaf', 'grid')), may hold values from -2 to 2
- couple_middle: float32 [4096, 128], P(('leaf', 'grid')), may hold values from -0.5 to 0.5
- ranks_middle: int32 [4, 2], replicated, may hold values from 32 to 128
- targets_middle: int32 [4096], P(('leaf', 'grid')), may hold values from 0 to 4095, as said below
- source_upper: float32 [8, 4096], P(None, ('leaf', 'grid')), may hold values from -6 to 6
- block_upper: float32 [4096, 128], P(('leaf', 'grid')), may hold values from -0.5 to 0.5
- expand_upper: float32 [4096, 128], P(('leaf', 'grid')), may hold values from -0.5 to 0.5
- basis_upper: float32 [4096, 256], P(('leaf', 'grid')), may hold values from -0.125 to 0.125
- pivot_upper: float32 [4096], P(('leaf', 'grid')), may hold values from -2 to 2
- couple_upper: float32 [4096, 128], P(('leaf', 'grid')), may hold values from -0.5 to 0.5
- ranks_upper: int32 [2, 2], replicated, may hold values from 32 to 128
- targets_upper: int32 [4096], P(('leaf', 'grid')), may hold values from 0 to 4095, as said below
- source_root: float32 [8, 4096], P(None, ('leaf', 'grid')), may hold values from -6 to 6
- block_root: float32 [4096, 128], P(('leaf', 'grid')), may hold values from -0.5 to 0.5
- expand_root: float32 [4096, 128], P(('leaf', 'grid')), may hold values from -0.5 to 0.5
- basis_root: float32 [4096, 256], P(('leaf', 'grid')), may hold values from -0.09375 to 0.09375
- pivot_root: float32 [4096], P(('leaf', 'grid')), may hold values from -2 to 2
- ranks_root: int32 [1, 2], replicated, may hold values from 32 to 128
Outputs:
- answer_leaf: float32 [8, 4096], P(None, ('leaf', 'grid'))
- answer_middle: float32 [8, 4096], P(None, ('leaf', 'grid'))
- answer_upper: float32 [8, 4096], P(None, ('leaf', 'grid'))
- answer_root: float32 [8, 4096], P(None, ('leaf', 'grid'))
Inputs may be any that keep to these rules, and one draw needn't show every extreme that they name: `targets_leaf`: within one leaf front the 1024 entries are distinct; each names a row of the parent front's row vector of 2048 rows. Split that vector's separator part and its update part each evenly, in order, over the parent's devices (leaf then grid); then the rows of one device name at most 32 rows held by any one of them, and exactly that many for some. `targets_middle`: within one middle front the entries are distinct; each names a row of the parent front's row vector of 4096 rows. Split likewise over the parent's devices, the rows of one device name at most 8 rows held by any one of them, and exactly that many for some. `targets_upper`: within one upper front the entries are distinct; each names a row of the root separator. Split evenly in order over all devices, the rows of one device name at most 4 rows held by any one of them, and exactly that many for some.
All inputs are finite; a program needn't handle non-finite values.
Results may differ from a plain program's by a relative error of at most 0.0003.
Values sent between devices are 32-bit elements; how exact they have to be, the bound alone decides.
A program may use at most 128 MiB of HBM per device.

v0:
```python
import jax
import jax.numpy as jnp
from jax import lax
from jax.sharding import PartitionSpec as P

BLOCK = 128
RANK = 128
HIGH_PRECISION = lax.Precision.HIGHEST


def from_partner(value, axis, distance):
    mask = 2**distance
    pairs = [(source, source ^ mask) for source in range(lax.axis_size(axis))]
    return lax.ppermute(value, axis, pairs)


def mult(left, right):
    return jnp.dot(left, right, precision=HIGH_PRECISION, preferred_element_type=jnp.float32)


def inner(left, right):
    return lax.dot_general(
        left,
        right,
        (((0,), (0,)), ((), ())),
        precision=HIGH_PRECISION,
        preferred_element_type=jnp.float32,
    )


def outer(left, right):
    return lax.dot_general(
        left,
        right,
        (((1,), (1,)), ((), ())),
        precision=HIGH_PRECISION,
        preferred_element_type=jnp.float32,
    )


def paired_total(partial_value, bits):
    summed = lax.psum(partial_value, "grid")
    for bit in range(bits):
        summed = summed + from_partner(summed, "leaf", bit)
    return summed


def group_total(partial_value, bits):
    return paired_total(partial_value, bits)


def upper_bit(place, bit):
    return place // (1 << bit) % 2 == 1


def group_extend(stack, bits, place):
    for bit in reversed(range(bits)):
        half = stack.shape[2] // 2
        lower_part = stack[:, :, :half]
        upper_part = stack[:, :, half:]
        flag = upper_bit(place, bit)
        keep = jnp.where(flag, upper_part, lower_part)
        send = jnp.where(flag, lower_part, upper_part)
        stack = keep + from_partner(send, "leaf", bit)
    return lax.psum_scatter(stack, "grid", scatter_dimension=2, tiled=True)


def group_fetch(stack, bits, place):
    current = lax.all_gather(stack, "grid", axis=2, tiled=True)
    for bit in range(bits):
        other = from_partner(current, "leaf", bit)
        flag = upper_bit(place, bit)
        current = jnp.where(
            flag,
            jnp.concatenate([other, current], axis=2),
            jnp.concatenate([current, other], axis=2),
        )
    return current


def forward_level(source, incoming, block, expand, basis, pivot, ranks, bits, front):
    level_batch_index = source if incoming is None else source + incoming
    count, width = level_batch_index.shape
    tiles = block.reshape(width // BLOCK, BLOCK, BLOCK)
    local_portion = jnp.einsum(
        "anh,nhk->ank",
        level_batch_index.reshape(count, width // BLOCK, BLOCK),
        tiles,
        precision=HIGH_PRECISION,
    ).reshape(count, width)
    query_lookup = basis[:, :RANK]
    coupling_right_factor = basis[:, RANK:]
    rank_pair = lax.dynamic_index_in_dim(ranks, front, 0, keepdims=False)
    columns = jnp.arange(RANK, dtype=jnp.int32)
    head_mask_grid = (columns < rank_pair[0]).astype(jnp.float32)
    column_mask_grid = (columns < rank_pair[1]).astype(jnp.float32)
    partial_value = jnp.concatenate(
        [
            mult(level_batch_index, query_lookup),
            mult(local_portion, coupling_right_factor),
            inner(expand, coupling_right_factor),
        ],
        axis=0,
    )
    total = group_total(partial_value, bits)
    hidden_q = total[:count] * head_mask_grid
    cross = total[2 * count :]
    intermediate_entries = local_portion + outer(hidden_q, expand)
    weight_entries = (total[count : 2 * count] + mult(hidden_q, cross)) * column_mask_grid
    return (
        intermediate_entries * pivot[None, :],
        weight_entries,
        (tiles, query_lookup, coupling_right_factor, cross, head_mask_grid, column_mask_grid),
    )


def backward_level(correction_entries, x_upd, couple, expand, parts, bits):
    tiles, query_lookup, coupling_right_factor, cross, head_mask_grid, column_mask_grid = parts
    count, width = correction_entries.shape
    if x_upd is None:
        total = group_total(mult(correction_entries, expand), bits)
        remainder_rows = correction_entries
        right_projection = total * head_mask_grid
    else:
        total = group_total(
            jnp.concatenate([mult(x_upd, couple), mult(correction_entries, expand)], axis=0), bits
        )
        solve_direction = total[:count] * column_mask_grid
        remainder_rows = correction_entries - outer(solve_direction, coupling_right_factor)
        right_projection = (total[count:] - outer(solve_direction, cross)) * head_mask_grid
    local_portion = jnp.einsum(
        "anh,nkh->ank",
        remainder_rows.reshape(count, width // BLOCK, BLOCK),
        tiles,
        precision=HIGH_PRECISION,
    ).reshape(count, width)
    return local_portion + outer(right_projection, query_lookup)


def extend(update, targets, sep_total, has_update, bits, place):
    count = update.shape[0]
    pieces = 2 if has_update else 1
    rows = sep_total * pieces
    buffer = jnp.zeros((count, rows), jnp.float32).at[:, targets].add(update)
    if has_update:
        stack = jnp.stack([buffer[:, :sep_total], buffer[:, sep_total:]])
    else:
        stack = buffer[None]
    return group_extend(stack, bits, place)


def fetch(stack, targets, bits, place):
    front_full = group_fetch(stack, bits, place)
    rows = front_full.transpose(1, 0, 2).reshape(front_full.shape[1], -1)
    return jnp.take(rows, targets, axis=1)


def shards(
    source_leaf,
    block_leaf,
    expand_leaf,
    basis_leaf,
    pivot_leaf,
    couple_leaf,
    ranks_leaf,
    targets_leaf,
    source_middle,
    block_middle,
    expand_middle,
    basis_middle,
    pivot_middle,
    couple_middle,
    ranks_middle,
    targets_middle,
    source_upper,
    block_upper,
    expand_upper,
    basis_upper,
    pivot_upper,
    couple_upper,
    ranks_upper,
    targets_upper,
    source_root,
    block_root,
    expand_root,
    basis_root,
    pivot_root,
    ranks_root,
):
    levels = [
        (
            source_leaf,
            block_leaf,
            expand_leaf,
            basis_leaf,
            pivot_leaf,
            couple_leaf,
            ranks_leaf,
            targets_leaf,
        ),
        (
            source_middle,
            block_middle,
            expand_middle,
            basis_middle,
            pivot_middle,
            couple_middle,
            ranks_middle,
            targets_middle,
        ),
        (
            source_upper,
            block_upper,
            expand_upper,
            basis_upper,
            pivot_upper,
            couple_upper,
            ranks_upper,
            targets_upper,
        ),
        (source_root, block_root, expand_root, basis_root, pivot_root, None, ranks_root, None),
    ]
    leaves = lax.axis_size("leaf")
    across = lax.axis_size("grid")
    place = lax.axis_index("leaf")
    depth = leaves.bit_length() - 1
    groups = [1, leaves // 4, leaves // 2, leaves]
    bit_counts = [0, depth - 2, depth - 1, depth]
    owners = [place // groups[level] for level in range(4)]
    inc_sep = None
    inc_upd = None
    saved = []
    for level in range(4):
        source, block, expand, basis, pivot, couple, ranks, targets = levels[level]
        correction_entries, weight_entries, parts = forward_level(
            source, inc_sep, block, expand, basis, pivot, ranks, bit_counts[level], owners[level]
        )
        saved.append((correction_entries, parts))
        if level < 3:
            update = -outer(weight_entries, couple)
            if inc_upd is not None:
                update = update + inc_upd
            sep_total = levels[level + 1][0].shape[1] * across * groups[level + 1]
            has_update = level + 1 < 3
            stack = extend(update, targets, sep_total, has_update, bit_counts[level + 1], place)
            inc_sep = stack[0]
            inc_upd = stack[1] if has_update else None
    answers = [None, None, None, None]
    parent_stack = None
    for level in (3, 2, 1, 0):
        correction_entries, parts = saved[level]
        couple = levels[level][5]
        expand = levels[level][2]
        targets = levels[level][7]
        x_upd = None
        if level < 3:
            x_upd = fetch(parent_stack, targets, bit_counts[level + 1], place)
        xvals = backward_level(correction_entries, x_upd, couple, expand, parts, bit_counts[level])
        answers[level] = xvals
        if level > 0:
            parent_stack = xvals[None] if x_upd is None else jnp.stack([xvals, x_upd])
    return (answers[0], answers[1], answers[2], answers[3])


def solution(mesh):
    in_specs = (
        P(None, ("leaf", "grid")),
        P(("leaf", "grid"), None),
        P(("leaf", "grid"), None),
        P(("leaf", "grid"), None),
        P(("leaf", "grid")),
        P(("leaf", "grid"), None),
        P(),
        P(("leaf", "grid")),
        P(None, ("leaf", "grid")),
        P(("leaf", "grid"), None),
        P(("leaf", "grid"), None),
        P(("leaf", "grid"), None),
        P(("leaf", "grid")),
        P(("leaf", "grid"), None),
        P(),
        P(("leaf", "grid")),
        P(None, ("leaf", "grid")),
        P(("leaf", "grid"), None),
        P(("leaf", "grid"), None),
        P(("leaf", "grid"), None),
        P(("leaf", "grid")),
        P(("leaf", "grid"), None),
        P(),
        P(("leaf", "grid")),
        P(None, ("leaf", "grid")),
        P(("leaf", "grid"), None),
        P(("leaf", "grid"), None),
        P(("leaf", "grid"), None),
        P(("leaf", "grid")),
        P(),
    )
    out_specs = (
        P(None, ("leaf", "grid")),
        P(None, ("leaf", "grid")),
        P(None, ("leaf", "grid")),
        P(None, ("leaf", "grid")),
    )
    return jax.shard_map(shards, mesh=mesh, in_specs=in_specs, out_specs=out_specs, check_vma=False)
```

profile of v0, /device:TPU:0, one launch (start us, length us, event | category | flops | bytes accessed | tf_op | source)
XLA Modules:
  0.0 397.3 jit_solution(7661426514770940477)
XLA Ops:
  17.3 27.4 %all-reduce.5.cloned.1.call-done = f32[144,128]{1,0:T(8,128)} async-done(((f32[144,128]{1,0:T(8,128)}), f32[144,128]{1,0:T(8,128)}) %all-reduce.5.cloned.1.call-update) | async-done | bytes 73744 | tf_op jit(solution)/shard_map/psum | solution.py:42
  46.1 1.7 scatter_custom_fusion
  48.2 1.9 collective-permute-start
  50.2 2.0 collective-permute-done
  53.4 21.0 %reduce-scatter.4.cloned.1.call-done = f32[2,8,128]{2,1,0:T(8,128)} async-done(((f32[2,8,512]{2,1,0:T(8,128)}), f32[2,8,128]{2,1,0:T(8,128)}) %reduce-scatter.4.cloned.1.call-update) | async-done | bytes 8208 | tf_op jit(solution)/shard_map/reduce_scatter | solution.py:65
  77.7 29.1 %all-reduce.7.cloned.1.call-done = f32[144,128]{1,0:T(8,128)} async-done(((f32[144,128]{1,0:T(8,128)}), f32[144,128]{1,0:T(8,128)}) %all-reduce.7.cloned.1.call-update) | async-done | bytes 73744 | tf_op jit(solution)/shard_map/psum | solution.py:42
  106.8 1.9 collective-permute-start.1
  109.3 2.3 collective-permute-done.1
  114.2 1.5 scatter_custom_fusion.1
  117.0 1.6 copy.75
  118.9 1.8 collective-permute-start.2
  121.1 2.2 collective-permute-done.2
  123.3 1.8 collective-permute-start.3
  125.1 2.2 collective-permute-done.3
  128.0 21.2 %reduce-scatter.6.cloned.1.call-done = f32[2,8,128]{2,1,0:T(8,128)} async-done(((f32[2,8,512]{2,1,0:T(8,128)}), f32[2,8,128]{2,1,0:T(8,128)}) %reduce-scatter.6.cloned.1.call-update) | async-done | bytes 8208 | tf_op jit(solution)/shard_map/reduce_scatter | solution.py:65
  152.4 29.2 %all-reduce.9.cloned.1.call-done = f32[144,128]{1,0:T(8,128)} async-done(((f32[144,128]{1,0:T(8,128)}), f32[144,128]{1,0:T(8,128)}) %all-reduce.9.cloned.1.call-update) | async-done | bytes 73744 | tf_op jit(solution)/shard_map/psum | solution.py:42
  181.6 1.9 collective-permute-start.4
  184.1 2.3 collective-permute-done.4
  187.4 1.8 collective-permute-start.5
  189.9 1.9 collective-permute-done.5
  193.5 1.5 scatter_custom_fusion.2
  196.0 2.7 collective-permute-start.6
  198.7 2.8 collective-permute-done.6
  203.0 1.8 collective-permute-start.7
  205.2 9.0 %collective-permute-done.7 = f32[1,8,1024]{1,2,0:T(8,128)S(1)} collective-permute-done((f32[1,8,1024]{1,2,0:T(8,128)S(1)}, f32[1,8,1024]{1,2,0:T(8,128)S(1)}, u32[]{:S(2)}, u32[]{:S(2)}) %collective-permute-start.7) | collective-permute-done | bytes 32800 | tf_op jit(solution)/shard_map/ppermute | solution.py:14
  214.4 1.7 collective-permute-start.8
  216.7 4.2 %collective-permute-done.8 = f32[1,8,512]{1,2,0:T(8,128)S(1)} collective-permute-done((f32[1,8,512]{1,2,0:T(8,128)S(1)}, f32[1,8,512]{1,2,0:T(8,128)S(1)}, u32[]{:S(2)}, u32[]{:S(2)}) %collective-permute-start.8) | collective-permute-done | bytes 16416 | tf_op jit(solution)/shard_map/ppermute | solution.py:14
  222.3 20.4 %reduce-scatter.8.cloned.1.call-done = f32[1,8,128]{1,2,0:T(8,128)} async-done(((f32[1,8,512]{1,2,0:T(8,128)}), f32[1,8,128]{1,2,0:T(8,128)}) %reduce-scatter.8.cloned.1.call-update) | async-done | bytes 4112 | tf_op jit(solution)/shard_map/reduce_scatter | solution.py:65
  246.3 29.2 %all-reduce.11.cloned.1.call-done = f32[144,128]{1,0:T(8,128)} async-done(((f32[144,128]{1,0:T(8,128)}), f32[144,128]{1,0:T(8,128)}) %all-reduce.11.cloned.1.call-update) | async-done | bytes 73744 | tf_op jit(solution)/shard_map/psum | solution.py:42
  275.5 1.9 collective-permute-start.9
  277.4 3.0 collective-permute-done.9
  281.3 1.8 collective-permute-start.10
  283.1 2.6 collective-permute-done.10
  285.7 2.7 collective-permute-start.11
  288.5 2.5 collective-permute-done.11
  291.4 5.9 %psum.60 = f32[8,128]{1,0:T(8,128)S(1)} all-reduce(f32[8,128]{1,0:T(8,128)S(1)} %fusion.123), channel_id=1, replica_groups=mesh['leaf'=8,'grid'=4] {'grid'}, use_global_device_ids=true, to_apply=%region_10.11 | all-reduce | flops 1024 | bytes 8192 | tf_op jit(solution)/shard_map/psum | solution.py:42
  297.4 1.5 collective-permute-start.12
  298.9 2.1 collective-permute-done.12
  301.0 1.5 collective-permute-start.13
  302.7 1.9 collective-permute-done.13
  304.6 3.0 collective-permute-start.14
  307.8 1.4 collective-permute-done.14
  309.4 5.6 %all-gather = f32[8,512]{1,0:T(8,128)S(1)} all-gather(f32[8,128]{1,0:T(8,128)S(1)} %convolution_add_fusion.3), channel_id=2, replica_groups=mesh['leaf'=8,'grid'=4] {'grid'}, dimensions={1}, use_global_device_ids=true | all-gather | bytes 20480 | tf_op jit(solution)/shard_map/all_gather | solution.py:69
  314.9 1.5 collective-permute-start.15
  316.6 2.1 collective-permute-done.15
  318.7 1.5 collective-permute-start.16
  320.2 2.4 collective-permute-done.16
  322.6 3.0 collective-permute-start.17
  325.6 2.2 collective-permute-done.17
  330.0 5.8 %psum.61 = f32[16,128]{1,0:T(8,128)S(1)} all-reduce(f32[16,128]{1,0:T(8,128)S(1)} %pad_maximum_fusion.6), channel_id=1, replica_groups=mesh['leaf'=8,'grid'=4] {'grid'}, use_global_device_ids=true, to_apply=%region_11.13 | all-reduce | flops 2048 | bytes 16384 | tf_op jit(solution)/shard_map/psum | solution.py:42
  335.8 1.5 collective-permute-start.18
  339.5 1.7 collective-permute-start.19
  346.0 5.5 %all_gather.10 = f32[2,8,512]{2,1,0:T(8,128)S(1)} all-gather(f32[2,8,128]{2,1,0:T(8,128)S(1)} %pad_maximum_fusion.7), channel_id=1, replica_groups=mesh['leaf'=8,'grid'=4] {'grid'}, dimensions={2}, use_global_device_ids=true | all-gather | bytes 40960 | tf_op jit(solution)/shard_map/all_gather | solution.py:69
  351.5 1.5 collective-permute-start.20
  353.2 2.2 collective-permute-done.20
  355.4 1.8 collective-permute-start.21
  357.3 2.4 collective-permute-done.21
  361.3 5.8 %psum.62 = f32[16,128]{1,0:T(8,128)S(1)} all-reduce(f32[16,128]{1,0:T(8,128)S(1)} %pad_maximum_fusion.8), channel_id=1, replica_groups=mesh['leaf'=8,'grid'=4] {'grid'}, use_global_device_ids=true, to_apply=%region_12.14 | all-reduce | flops 2048 | bytes 16384 | tf_op jit(solution)/shard_map/psum | solution.py:42
  367.1 1.5 collective-permute-start.22
  368.6 2.2 collective-permute-done.22
  371.7 5.3 %all_gather.11 = f32[2,8,512]{2,1,0:T(8,128)S(1)} all-gather(f32[2,8,128]{2,1,0:T(8,128)S(1)} %pad_maximum_fusion.9), channel_id=1, replica_groups=mesh['leaf'=8,'grid'=4] {'grid'}, dimensions={2}, use_global_device_ids=true | all-gather | bytes 40960 | tf_op jit(solution)/shard_map/all_gather | solution.py:69
  377.0 1.5 collective-permute-start.23
  378.6 2.3 collective-permute-done.23
  382.4 6.5 %psum.63 = f32[16,128]{1,0:T(8,128)S(1)} all-reduce(f32[16,128]{1,0:T(8,128)S(1)} %pad_maximum_fusion.10), channel_id=1, replica_groups=mesh['leaf'=8,'grid'=4] {'grid'}, use_global_device_ids=true, to_apply=%region_13.15 | all-reduce | flops 2048 | bytes 16384 | tf_op jit(solution)/shard_map/psum | solution.py:42
  (264 shorter events, 54.5 us)
Async XLA Ops:
  7.2 38.5 %copy-start = (f32[256,128]{1,0:T(8,128)S(1)}, f32[256,128]{1,0:T(8,128)}, u32[]{:S(2)}) copy-start(f32[256,128]{1,0:T(8,128)} %param.37) | copy-start | bytes 393220
  7.2 37.5 %all-reduce.5.cloned.1.call-start = ((), (), s32[]{:S(2)}) async-start(), calls=%async_computation.3 | async-start | bytes 147456 | tf_op jit(solution)/shard_map/psum | solution.py:42
  12.1 62.3 %reduce-scatter.4.cloned.1.call-start = ((), (), s32[]{:S(2)}) async-start(), calls=%async_computation.4 | async-start | bytes 40960 | tf_op jit(solution)/shard_map/reduce_scatter | solution.py:65
  14.1 33.9 %copy-start.42 = (s32[256]{0:T(256)}, s32[256]{0:T(256)S(1)}, u32[]{:S(2)}) copy-start(s32[256]{0:T(256)S(1)} %compare_select_fusion) | copy-start | bytes 3076
  14.8 99.4 %copy-start.50 = (s32[128]{0:T(128)}, s32[128]{0:T(128)S(1)}, u32[]{:S(2)}) copy-start(s32[128]{0:T(128)S(1)} %compare_select_fusion.1) | copy-start | bytes 1540
  47.8 65.4 %copy-start.20 = (f32[128,128]{1,0:T(8,128)S(1)}, f32[128,128]{1,0:T(8,128)}, u32[]{:S(2)}) copy-start(f32[128,128]{1,0:T(8,128)} %param.45) | copy-start | bytes 196612
  48.2 4.0 collective-permute-start
  52.8 54.0 %all-reduce.7.cloned.1.call-start = ((), (), s32[]{:S(2)}) async-start(), calls=%async_computation.5 | async-start | bytes 147456 | tf_op jit(solution)/shard_map/psum | solution.py:42
  77.0 72.3 %reduce-scatter.6.cloned.1.call-start = ((), (), s32[]{:S(2)}) async-start(), calls=%async_computation.6 | async-start | bytes 40960 | tf_op jit(solution)/shard_map/reduce_scatter | solution.py:65
  77.7 39.2 %copy-start.34 = (f32[128]{0:T(128)}, f32[128]{0:T(128)S(1)}, u32[]{:S(2)}) copy-start(f32[128]{0:T(128)S(1)} %compare_convert_fusion.4) | copy-start | bytes 1540
  106.8 4.9 %collective-permute-start.1 = (f32[144,128]{1,0:T(8,128)}, f32[144,128]{1,0:T(8,128)S(1)}, u32[]{:S(2)}, u32[]{:S(2)}) collective-permute-start(f32[144,128]{1,0:T(8,128)} %all-reduce.7.cloned.1.call-done), channel_id=1, source_target_pairs={{0,4},{4,0},{8,12},{12,8},{16,20},{20,16},{24,28},{28,24},{1,5},{5... | collective-permute-start | bytes 221192 | tf_op jit(solution)/shard_map/ppermute | solution.py:14
  117.0 75.5 %copy-start.18 = (f32[128,128]{1,0:T(8,128)S(1)}, f32[128,128]{1,0:T(8,128)}, u32[]{:S(2)}) copy-start(f32[128,128]{1,0:T(8,128)} %param.53) | copy-start | bytes 196612
  118.9 4.3 %collective-permute-start.2 = (f32[2,8,1024]{2,1,0:T(8,128)S(1)}, f32[2,8,1024]{2,1,0:T(8,128)S(1)}, u32[]{:S(2)}, u32[]{:S(2)}) collective-permute-start(f32[2,8,1024]{2,1,0:T(8,128)S(1)} %broadcast_select_fusion), channel_id=1, source_target_pairs={{0,8},{4,12},{8,0},{12,4},{16,24},{20,28},{24,16},{28,20},{1,9},{5... | collective-permute-start | bytes 196616 | tf_op jit(solution)/shard_map/ppermute | solution.py:14
  123.3 4.0 %collective-permute-start.3 = (f32[2,8,512]{2,1,0:T(8,128)S(1)}, f32[2,8,512]{2,1,0:T(8,128)S(1)}, u32[]{:S(2)}, u32[]{:S(2)}) collective-permute-start(f32[2,8,512]{2,1,0:T(8,128)S(1)} %slice_select_fusion.3), channel_id=1, source_target_pairs={{0,4},{4,0},{8,12},{12,8},{16,20},{20,16},{24,28},{28,24},{1,5},{5... | collective-permute-start | bytes 98312 | tf_op jit(solution)/shard_map/ppermute | solution.py:14
  125.1 69.9 %copy-start.52 = (s32[128]{0:T(128)}, s32[128]{0:T(128)S(1)}, u32[]{:S(2)}) copy-start(s32[128]{0:T(128)S(1)} %compare_select_fusion.2) | copy-start | bytes 1540
  127.9 53.7 %all-reduce.9.cloned.1.call-start = ((), (), s32[]{:S(2)}) async-start(), calls=%async_computation.7 | async-start | bytes 147456 | tf_op jit(solution)/shard_map/psum | solution.py:42
  151.8 90.8 %reduce-scatter.8.cloned.1.call-start = ((), (), s32[]{:S(2)}) async-start(), calls=%async_computation.8 | async-start | bytes 327680 | tf_op jit(solution)/shard_map/reduce_scatter | solution.py:65
  181.6 4.9 %collective-permute-start.4 = (f32[144,128]{1,0:T(8,128)}, f32[144,128]{1,0:T(8,128)S(1)}, u32[]{:S(2)}, u32[]{:S(2)}) collective-permute-start(f32[144,128]{1,0:T(8,128)} %all-reduce.9.cloned.1.call-done), channel_id=1, source_target_pairs={{0,4},{4,0},{8,12},{12,8},{16,20},{20,16},{24,28},{28,24},{1,5},{5... | collective-permute-start | bytes 221192 | tf_op jit(solution)/shard_map/ppermute | solution.py:14
  187.4 4.4 %collective-permute-start.5 = (f32[144,128]{1,0:T(8,128)S(1)}, f32[144,128]{1,0:T(8,128)S(1)}, u32[]{:S(2)}, u32[]{:S(2)}) collective-permute-start(f32[144,128]{1,0:T(8,128)S(1)} %add.207), channel_id=1, source_target_pairs={{0,8},{4,12},{8,0},{12,4},{16,24},{20,28},{24,16},{28,20},{1,9},{5... | collective-permute-start | bytes 221192 | tf_op jit(solution)/shard_map/ppermute | solution.py:14
  196.0 5.5 %collective-permute-start.6 = (f32[1,8,2048]{2,1,0:T(8,128)}, f32[1,8,2048]{2,1,0:T(8,128)}, u32[]{:S(2)}, u32[]{:S(2)}) collective-permute-start(f32[1,8,2048]{2,1,0:T(8,128)} %copy.65), channel_id=1, source_target_pairs={{0,16},{4,20},{8,24},{12,28},{16,0},{20,4},{24,8},{28,12},{1,17},{... | collective-permute-start | bytes 196616 | tf_op jit(solution)/shard_map/ppermute | solution.py:14
  203.0 11.2 %collective-permute-start.7 = (f32[1,8,1024]{1,2,0:T(8,128)S(1)}, f32[1,8,1024]{1,2,0:T(8,128)S(1)}, u32[]{:S(2)}, u32[]{:S(2)}) collective-permute-start(f32[1,8,1024]{1,2,0:T(8,128)S(1)} %slice_select_fusion.1), channel_id=1, source_target_pairs={{0,8},{4,12},{8,0},{12,4},{16,24},{20,28},{24,16},{28,20},{1,9},{5... | collective-permute-start | bytes 98312 | tf_op jit(solution)/shard_map/ppermute | solution.py:14
  205.1 37.5 %copy-start.17 = (f32[128,128]{1,0:T(8,128)S(1)}, f32[128,128]{1,0:T(8,128)}, u32[]{:S(2)}) copy-start(f32[128,128]{1,0:T(8,128)} %param.57) | copy-start | bytes 196612
  205.1 38.6 %copy-start.15 = (f32[128,256]{1,0:T(8,128)S(1)}, f32[128,256]{1,0:T(8,128)}, u32[]{:S(2)}) copy-start(f32[128,256]{1,0:T(8,128)} %param.59) | copy-start | bytes 393220
  205.1 40.5 %copy-start.58 = (s32[128]{0:T(128)S(1)}, s32[128]{0:T(128)}, u32[]{:S(2)}) copy-start(s32[128]{0:T(128)} %param.47) | copy-start | bytes 1540
  205.1 72.2 %copy-start.53 = (s32[128]{0:T(128)S(1)}, s32[128]{0:T(128)}, u32[]{:S(2)}) copy-start(s32[128]{0:T(128)} %copy-done.52) | copy-start | bytes 1540
  205.1 77.9 %copy-start.51 = (s32[128]{0:T(128)S(1)}, s32[128]{0:T(128)}, u32[]{:S(2)}) copy-start(s32[128]{0:T(128)} %copy-done.50) | copy-start | bytes 1540
  214.3 74.2 %copy-start.59 = (s32[1,2]{1,0:T(1,128)S(1)}, s32[1,2]{1,0:T(1,128)}, u32[]{:S(2)}) copy-start(s32[1,2]{1,0:T(1,128)} %param.61) | copy-start | bytes 28
  214.3 76.8 %copy-start.9 = (f32[128,128]{1,0:T(8,128)S(1)}, f32[128,128]{1,0:T(8,128)}, u32[]{:S(2)}) copy-start(f32[128,128]{1,0:T(8,128)} %param.58) | copy-start | bytes 196612
  214.3 76.8 %copy-start.54 = (f32[128]{0:T(128)S(1)}, f32[128]{0:T(128)}, u32[]{:S(2)}) copy-start(f32[128]{0:T(128)} %param.60) | copy-start | bytes 1540
  214.3 84.6 %copy-start.43 = (s32[256]{0:T(256)S(1)}, s32[256]{0:T(256)}, u32[]{:S(2)}) copy-start(s32[256]{0:T(256)} %copy-done.42) | copy-start | bytes 3076
  214.3 88.2 %copy-start.7 = (f32[144,128]{1,0:T(8,128)S(1)}, f32[144,128]{1,0:T(8,128)}, u32[]{:S(2)}) copy-start(f32[144,128]{1,0:T(8,128)} %copy-done.6) | copy-start | bytes 221188
  214.3 88.2 %copy-start.11 = (f32[128,128]{1,0:T(8,128)S(1)}, f32[128,128]{1,0:T(8,128)}, u32[]{:S(2)}) copy-start(f32[128,128]{1,0:T(8,128)} %param.50) | copy-start | bytes 196612
  214.3 88.2 %copy-start.39 = (f32[128]{0:T(128)S(1)}, f32[128]{0:T(128)}, u32[]{:S(2)}) copy-start(f32[128]{0:T(128)} %copy-done.38) | copy-start | bytes 1540
  214.3 88.2 %copy-start.47 = (f32[128]{0:T(128)S(1)}, f32[128]{0:T(128)}, u32[]{:S(2)}) copy-start(f32[128]{0:T(128)} %param.52) | copy-start | bytes 1540
  214.4 6.4 %collective-permute-start.8 = (f32[1,8,512]{1,2,0:T(8,128)S(1)}, f32[1,8,512]{1,2,0:T(8,128)S(1)}, u32[]{:S(2)}, u32[]{:S(2)}) collective-permute-start(f32[1,8,512]{1,2,0:T(8,128)S(1)} %slice_select_fusion.2), channel_id=1, source_target_pairs={{0,4},{4,0},{8,12},{12,8},{16,20},{20,16},{24,28},{28,24},{1,5},{5... | collective-permute-start | bytes 49160 | tf_op jit(solution)/shard_map/ppermute | solution.py:14
  221.6 53.9 %all-reduce.11.cloned.1.call-start = ((), (), s32[]{:S(2)}) async-start(), calls=%async_computation.9 | async-start | bytes 147456 | tf_op jit(solution)/shard_map/psum | solution.py:42
  244.9 84.3 %copy-start.19 = (f32[128,128]{1,0:T(8,128)S(1)}, f32[128,128]{1,0:T(8,128)}, u32[]{:S(2)}) copy-start(f32[128,128]{1,0:T(8,128)} %param.53) | copy-start | bytes 196612
  245.6 91.7 %copy-start.13 = (f32[128,128]{1,0:T(8,128)S(1)}, f32[128,128]{1,0:T(8,128)}, u32[]{:S(2)}) copy-start(f32[128,128]{1,0:T(8,128)} %param.34) | copy-start | bytes 196612
  245.6 91.7 %copy-start.16 = (f32[144,128]{1,0:T(8,128)S(1)}, f32[144,128]{1,0:T(8,128)}, u32[]{:S(2)}) copy-start(f32[144,128]{1,0:T(8,128)} %all-reduce.5.cloned.1.call-done) | copy-start | bytes 221188
  245.6 91.7 %copy-start.33 = (f32[128]{0:T(128)S(1)}, f32[128]{0:T(128)}, u32[]{:S(2)}) copy-start(f32[128]{0:T(128)} %copy-done.32) | copy-start | bytes 1540
  275.5 4.9 %collective-permute-start.9 = (f32[144,128]{1,0:T(8,128)}, f32[144,128]{1,0:T(8,128)S(1)}, u32[]{:S(2)}, u32[]{:S(2)}) collective-permute-start(f32[144,128]{1,0:T(8,128)} %all-reduce.11.cloned.1.call-done), channel_id=1, source_target_pairs={{0,4},{4,0},{8,12},{12,8},{16,20},{20,16},{24,28},{28,24},{1,5},{5... | collective-permute-start | bytes 221192 | tf_op jit(solution)/shard_map/ppermute | solution.py:14
  281.3 63.6 %copy-start.23 = (f32[128,128]{1,0:T(8,128)S(1)}, f32[128,128]{1,0:T(8,128)}, u32[]{:S(2)}) copy-start(f32[128,128]{1,0:T(8,128)} %param.49) | copy-start | bytes 196612
  281.3 4.4 %collective-permute-start.10 = (f32[144,128]{1,0:T(8,128)S(1)}, f32[144,128]{1,0:T(8,128)S(1)}, u32[]{:S(2)}, u32[]{:S(2)}) collective-permute-start(f32[144,128]{1,0:T(8,128)S(1)} %add.219), channel_id=1, source_target_pairs={{0,8},{4,12},{8,0},{12,4},{16,24},{20,28},{24,16},{28,20},{1,9},{5... | collective-permute-start | bytes 221192 | tf_op jit(solution)/shard_map/ppermute | solution.py:14
  285.7 67.3 %copy-start.5 = (f32[144,128]{1,0:T(8,128)S(1)}, f32[144,128]{1,0:T(8,128)}, u32[]{:S(2)}) copy-start(f32[144,128]{1,0:T(8,128)} %copy-done.4) | copy-start | bytes 221188
  285.7 67.3 %copy-start.12 = (f32[128,128]{1,0:T(8,128)S(1)}, f32[128,128]{1,0:T(8,128)}, u32[]{:S(2)}) copy-start(f32[128,128]{1,0:T(8,128)} %param.42) | copy-start | bytes 196612
  285.7 67.3 %copy-start.35 = (f32[128]{0:T(128)S(1)}, f32[128]{0:T(128)}, u32[]{:S(2)}) copy-start(f32[128]{0:T(128)} %copy-done.34) | copy-start | bytes 1540
  285.7 67.3 %copy-start.48 = (f32[128]{0:T(128)S(1)}, f32[128]{0:T(128)}, u32[]{:S(2)}) copy-start(f32[128]{0:T(128)} %param.44) | copy-start | bytes 1540
  285.7 5.3 %collective-permute-start.11 = (f32[144,128]{1,0:T(8,128)S(1)}, f32[144,128]{1,0:T(8,128)S(1)}, u32[]{:S(2)}, u32[]{:S(2)}) collective-permute-start(f32[144,128]{1,0:T(8,128)S(1)} %add.220), channel_id=1, source_target_pairs={{0,16},{4,20},{8,24},{12,28},{16,0},{20,4},{24,8},{28,12},{1,17},{... | collective-permute-start | bytes 221192 | tf_op jit(solution)/shard_map/ppermute | solution.py:14
  297.4 3.6 collective-permute-start.12
  301.0 3.6 collective-permute-start.13
  304.6 4.6 %collective-permute-start.14 = (f32[8,128]{1,0:T(8,128)S(1)}, f32[8,128]{1,0:T(8,128)S(1)}, u32[]{:S(2)}, u32[]{:S(2)}) collective-permute-start(f32[8,128]{1,0:T(8,128)S(1)} %add.224), channel_id=1, source_target_pairs={{0,16},{4,20},{8,24},{12,28},{16,0},{20,4},{24,8},{28,12},{1,17},{... | collective-permute-start | bytes 12296 | tf_op jit(solution)/shard_map/ppermute | solution.py:14
  309.4 50.4 %copy-start.29 = (f32[8,128]{1,0:T(8,128)}, f32[8,128]{1,0:T(8,128)S(1)}, u32[]{:S(2)}) copy-start(f32[8,128]{1,0:T(8,128)S(1)} %convolution_add_fusion.3) | copy-start | bytes 12292
  314.9 3.7 collective-permute-start.15
  318.7 3.9 collective-permute-start.16
  322.6 5.2 %collective-permute-start.17 = (f32[1,8,2048]{2,1,0:T(8,128)S(1)}, f32[1,8,2048]{2,1,0:T(8,128)S(1)}, u32[]{:S(2)}, u32[]{:S(2)}) collective-permute-start(f32[1,8,2048]{2,1,0:T(8,128)S(1)} %maximum_select_fusion.2), channel_id=1, source_target_pairs={{0,16},{4,20},{8,24},{12,28},{16,0},{20,4},{24,8},{28,12},{1,17},{... | collective-permute-start | bytes 196616 | tf_op jit(solution)/shard_map/ppermute | solution.py:14
  328.5 42.3 %copy-start.37 = (f32[128]{0:T(128)S(1)}, f32[128]{0:T(128)}, u32[]{:S(2)}) copy-start(f32[128]{0:T(128)} %copy-done.36) | copy-start | bytes 1540
  328.5 42.7 %copy-start.25 = (f32[128,128]{1,0:T(8,128)S(1)}, f32[128,128]{1,0:T(8,128)}, u32[]{:S(2)}) copy-start(f32[128,128]{1,0:T(8,128)} %param.41) | copy-start | bytes 196612
  335.8 3.7 collective-permute-start.18
  339.5 3.7 collective-permute-start.19
  345.9 35.3 %copy-start.30 = (f32[8,128]{1,0:T(8,128)}, f32[8,128]{1,0:T(8,128)S(1)}, u32[]{:S(2)}) copy-start(f32[8,128]{1,0:T(8,128)S(1)} %convolution_add_fusion.2) | copy-start | bytes 12292
  351.5 3.9 collective-permute-start.20
  355.4 4.3 %collective-permute-start.21 = (f32[2,8,1024]{2,1,0:T(8,128)S(1)}, f32[2,8,1024]{2,1,0:T(8,128)S(1)}, u32[]{:S(2)}, u32[]{:S(2)}) collective-permute-start(f32[2,8,1024]{2,1,0:T(8,128)S(1)} %maximum_select_fusion.4), channel_id=1, source_target_pairs={{0,8},{4,12},{8,0},{12,4},{16,24},{20,28},{24,16},{28,20},{1,9},{5... | collective-permute-start | bytes 196616 | tf_op jit(solution)/shard_map/ppermute | solution.py:14
  367.1 3.7 collective-permute-start.22
  377.0 3.9 collective-permute-start.23
  (27 other events, 445.1 us)
Sparse Core Ops, SparseCore 0:
  12.2 32.3 all-reduce.4
  52.9 21.4 reduce-scatter.3
  77.1 29.6 all-reduce.6
  128.0 21.1 reduce-scatter.5
  151.9 29.6 all-reduce.8
  221.7 20.8 reduce-scatter.7
  245.8 29.6 all-reduce.10
where the time goes:
time: 398 us; the launch traced here: 397 us
  waiting for transfers between devices  239 us (60%)
  starting transfers between devices  45.5 us (11%)
  blocking collectives  40.3 us (10%)
  matrix products  24 us (6%)
  other arithmetic  20.3 us (5%)
  between operations  15.1 us (4%)
  local copies, waits for them, and re-layouts  13.5 us (3%)
    psum x4, waiting for transfers between devices, paired_total(): summed = lax.psum(partial_value, 'grid')  115 us
    reduce_scatter x3, waiting for transfers between devices, group_extend(): return lax.psum_scatter(stack, 'grid', scatter_dimension=2, tiled=True)  62.6 us
    ppermute x24, waiting for transfers between devices, from_partner(): return lax.ppermute(value, axis, pairs)  60.9 us
    ppermute x24, starting transfers between devices, from_partner(): return lax.ppermute(value, axis, pairs)  45.2 us
    psum x4, blocking collectives, paired_total(): summed = lax.psum(partial_value, 'grid')  24 us
    all_gather x3, blocking collectives, group_fetch(): current = lax.all_gather(stack, 'grid', axis=2, tiled=True)  16.4 us
    dot_general x18, matrix products, mult(): jnp.dot(left, right, precision=HIGH_PRECISION, preferred_element_type=jnp...  8.73 us
  transfers between devices with their start and end apart: 31, of which 31 were waited for; matrix products, arithmetic and copies ran while one was open for 3% of the time, Pallas kernels for 0%

commit v1 on v0

--- a/solution.py
+++ b/solution.py
@@ -39,7 +39,7 @@
 
 
 def paired_total(partial_value, bits):
-    summed = lax.psum(partial_value, "grid")
+    summed = jnp.sum(lax.all_gather(partial_value, "grid"), axis=0)
     for bit in range(bits):
         summed = summed + from_partner(summed, "leaf", bit)
     return summed

time: 398 us -> 289 us (0.73)
  waiting for transfers between devices: 239 us -> 122 us
  blocking collectives: 40.3 us -> 61.6 us
  other arithmetic: 20.3 us -> 12.2 us
    psum x4 -> x0, waiting for transfers between devices: 115 us -> none  [paired_total(): summed = lax.psum(partial_value, 'grid')]
    all_gather x0 -> x8, blocking collectives: none -> 45.8 us  [paired_total(): summed = jnp.sum(lax.all_gather(partial_value, 'grid'), axis=0)]
    psum x4 -> x0, blocking collectives: 24 us -> none  [paired_total(): summed = lax.psum(partial_value, 'grid')]
  transfers between devices with their start and end apart: 31 -> 27, of which waited for: 31 -> 27; matrix products, arithmetic and copies ran while one was open for 3% -> 3% of each run, Pallas kernels for 0% -> 0%
where the time goes in v1:
time: 289 us; the launch traced here: 288 us
  waiting for transfers between devices  122 us (42%)
  blocking collectives  61.6 us (21%)
  starting transfers between devices  41.7 us (14%)
  matrix products  21.9 us (8%)
  between operations  14.7 us (5%)
  local copies, waits for them, and re-layouts  14.2 us (5%)
  other arithmetic  12.2 us (4%)
    ppermute x24, waiting for transfers between devices, from_partner(): return lax.ppermute(value, axis, pairs)  61.6 us
    reduce_scatter x3, waiting for transfers between devices, group_extend(): return lax.psum_scatter(stack, 'grid', scatter_dimension=2, tiled=True)  60 us
    all_gather x8, blocking collectives, paired_total(): summed = jnp.sum(lax.all_gather(partial_value, 'grid'), axis=0)  45.8 us
    ppermute x24, starting transfers between devices, from_partner(): return lax.ppermute(value, axis, pairs)  41.6 us
    all_gather x3, blocking collectives, group_fetch(): current = lax.all_gather(stack, 'grid', axis=2, tiled=True)  15.8 us
    dot_general x18, matrix products, mult(): jnp.dot(left, right, precision=HIGH_PRECISION, preferred_element_type=jnp...  7.23 us
    dot_general x17, matrix products, outer(): lax.dot_general(left, right, (((1,), (1,)), ((), ())), precision=HIGH_PRE...  5.93 us
  transfers between devices with their start and end apart: 27, of which 27 were waited for; matrix products, arithmetic and copies ran while one was open for 3% of the time, Pallas kernels for 0%

profile of v1, /device:TPU:0, one launch (start us, length us, event | category | flops | bytes accessed | tf_op | source)
XLA Modules:
  0.0 287.9 jit_solution(18311446836549763083)
XLA Ops:
  12.7 7.4 %all-gather = f32[576,128]{1,0:T(8,128)S(1)} all-gather(f32[144,128]{1,0:T(8,128)S(1)} %pad_maximum_fusion), channel_id=2, replica_groups=mesh['leaf'=8,'grid'=4] {'grid'}, dimensions={0}, use_global_device_ids=true | all-gather | bytes 368640 | tf_op jit(solution)/shard_map/all_gather | solution.py:42
  23.4 1.7 scatter_custom_fusion
  25.5 1.6 collective-permute-start
  30.9 20.1 %reduce-scatter.4.cloned.1.call-done = f32[2,8,128]{2,1,0:T(8,128)} async-done(((f32[2,8,512]{2,1,0:T(8,128)}), f32[2,8,128]{2,1,0:T(8,128)}) %reduce-scatter.4.cloned.1.call-update) | async-done | bytes 8208 | tf_op jit(solution)/shard_map/reduce_scatter | solution.py:65
  52.9 5.9 %all-gather.1 = f32[576,128]{1,0:T(8,128)S(1)} all-gather(f32[144,128]{1,0:T(8,128)S(1)} %pad_maximum_fusion.1), channel_id=3, replica_groups=mesh['leaf'=8,'grid'=4] {'grid'}, dimensions={0}, use_global_device_ids=true | all-gather | bytes 368640 | tf_op jit(solution)/shard_map/all_gather | solution.py:42
  58.8 1.5 collective-permute-start.1
  61.0 2.4 collective-permute-done.1
  65.0 1.5 scatter_custom_fusion.1
  67.8 1.6 copy.75
  69.7 1.6 collective-permute-start.2
  71.3 2.8 collective-permute-done.2
  74.1 1.5 collective-permute-start.3
  75.6 2.4 collective-permute-done.3
  79.3 19.1 %reduce-scatter.6.cloned.1.call-done = f32[2,8,128]{2,1,0:T(8,128)} async-done(((f32[2,8,512]{2,1,0:T(8,128)}), f32[2,8,128]{2,1,0:T(8,128)}) %reduce-scatter.6.cloned.1.call-update) | async-done | bytes 8208 | tf_op jit(solution)/shard_map/reduce_scatter | solution.py:65
  100.3 5.9 %all-gather.2 = f32[576,128]{1,0:T(8,128)S(1)} all-gather(f32[144,128]{1,0:T(8,128)S(1)} %pad_maximum_fusion.2), channel_id=4, replica_groups=mesh['leaf'=8,'grid'=4] {'grid'}, dimensions={0}, use_global_device_ids=true | all-gather | bytes 368640 | tf_op jit(solution)/shard_map/all_gather | solution.py:42
  106.2 1.5 collective-permute-start.4
  108.4 2.4 collective-permute-done.4
  110.8 1.6 collective-permute-start.5
  113.0 2.2 collective-permute-done.5
  116.9 1.5 scatter_custom_fusion.2
  119.4 2.4 collective-permute-start.6
  121.8 1.8 fusion.32
  126.4 1.6 collective-permute-start.7
  128.9 8.6 %collective-permute-done.7 = f32[1,8,1024]{1,2,0:T(8,128)S(1)} collective-permute-done((f32[1,8,1024]{1,2,0:T(8,128)S(1)}, f32[1,8,1024]{1,2,0:T(8,128)S(1)}, u32[]{:S(2)}, u32[]{:S(2)}) %collective-permute-start.7) | collective-permute-done | bytes 32800 | tf_op jit(solution)/shard_map/ppermute | solution.py:14
  137.7 1.5 collective-permute-start.8
  139.4 4.8 %collective-permute-done.8 = f32[1,8,512]{1,2,0:T(8,128)S(1)} collective-permute-done((f32[1,8,512]{1,2,0:T(8,128)S(1)}, f32[1,8,512]{1,2,0:T(8,128)S(1)}, u32[]{:S(2)}, u32[]{:S(2)}) %collective-permute-start.8) | collective-permute-done | bytes 16416 | tf_op jit(solution)/shard_map/ppermute | solution.py:14
  145.1 20.8 %reduce-scatter.8.cloned.1.call-done = f32[1,8,128]{1,2,0:T(8,128)} async-done(((f32[1,8,512]{1,2,0:T(8,128)}), f32[1,8,128]{1,2,0:T(8,128)}) %reduce-scatter.8.cloned.1.call-update) | async-done | bytes 4112 | tf_op jit(solution)/shard_map/reduce_scatter | solution.py:65
  168.2 5.9 %all-gather.3 = f32[576,128]{1,0:T(8,128)S(1)} all-gather(f32[144,128]{1,0:T(8,128)S(1)} %pad_maximum_fusion.3), channel_id=5, replica_groups=mesh['leaf'=8,'grid'=4] {'grid'}, dimensions={0}, use_global_device_ids=true | all-gather | bytes 368640 | tf_op jit(solution)/shard_map/all_gather | solution.py:42
  174.1 1.6 collective-permute-start.9
  175.7 3.0 %collective-permute-done.9 = f32[144,128]{1,0:T(8,128)S(1)} collective-permute-done((f32[144,128]{1,0:T(8,128)S(1)}, f32[144,128]{1,0:T(8,128)S(1)}, u32[]{:S(2)}, u32[]{:S(2)}) %collective-permute-start.9) | collective-permute-done | bytes 73760 | tf_op jit(solution)/shard_map/ppermute | solution.py:14
  178.7 1.6 collective-permute-start.10
  180.3 2.8 collective-permute-done.10
  183.2 2.5 collective-permute-start.11
  185.8 2.8 collective-permute-done.11
  188.9 5.2 %all-gather.4 = f32[32,128]{1,0:T(8,128)S(1)} all-gather(f32[8,128]{1,0:T(8,128)S(1)} %fusion.123), channel_id=6, replica_groups=mesh['leaf'=8,'grid'=4] {'grid'}, dimensions={0}, use_global_device_ids=true | all-gather | bytes 20480 | tf_op jit(solution)/shard_map/all_gather | solution.py:42
  194.1 1.5 collective-permute-start.12
  195.6 2.1 collective-permute-done.12
  199.4 1.9 collective-permute-done.13
  201.4 2.7 collective-permute-start.14
  204.2 1.7 collective-permute-done.14
  206.0 5.4 %all-gather.5 = f32[8,512]{1,0:T(8,128)S(1)} all-gather(f32[8,128]{1,0:T(8,128)S(1)} %convolution_add_fusion.3), channel_id=7, replica_groups=mesh['leaf'=8,'grid'=4] {'grid'}, dimensions={1}, use_global_device_ids=true | all-gather | bytes 20480 | tf_op jit(solution)/shard_map/all_gather | solution.py:69
  211.5 1.5 collective-permute-start.15
  213.1 2.1 collective-permute-done.15
  215.2 1.8 collective-permute-start.16
  217.0 2.2 collective-permute-done.16
  219.1 2.7 collective-permute-start.17
  221.9 2.5 collective-permute-done.17
  225.9 5.2 %all-gather.6 = f32[64,128]{1,0:T(8,128)S(1)} all-gather(f32[16,128]{1,0:T(8,128)S(1)} %pad_maximum_fusion.6), channel_id=8, replica_groups=mesh['leaf'=8,'grid'=4] {'grid'}, dimensions={0}, use_global_device_ids=true | all-gather | bytes 40960 | tf_op jit(solution)/shard_map/all_gather | solution.py:42
  231.1 1.5 collective-permute-start.18
  232.6 2.1 collective-permute-done.18
  234.8 1.8 collective-permute-start.19
  236.5 1.9 collective-permute-done.19
  239.3 5.2 %all_gather.70 = f32[2,8,512]{2,1,0:T(8,128)S(1)} all-gather(f32[2,8,128]{2,1,0:T(8,128)S(1)} %pad_maximum_fusion.7), channel_id=1, replica_groups=mesh['leaf'=8,'grid'=4] {'grid'}, dimensions={2}, use_global_device_ids=true | all-gather | bytes 40960 | tf_op jit(solution)/shard_map/all_gather | solution.py:69
  244.5 1.5 collective-permute-start.20
  246.2 2.2 collective-permute-done.20
  248.4 1.8 collective-permute-start.21
  250.4 2.4 collective-permute-done.21
  254.3 5.2 %all-gather.7 = f32[64,128]{1,0:T(8,128)S(1)} all-gather(f32[16,128]{1,0:T(8,128)S(1)} %pad_maximum_fusion.8), channel_id=9, replica_groups=mesh['leaf'=8,'grid'=4] {'grid'}, dimensions={0}, use_global_device_ids=true | all-gather | bytes 40960 | tf_op jit(solution)/shard_map/all_gather | solution.py:42
  259.5 1.5 collective-permute-start.22
  261.0 2.2 collective-permute-done.22
  264.1 5.2 %all_gather.73 = f32[2,8,512]{2,1,0:T(8,128)S(1)} all-gather(f32[2,8,128]{2,1,0:T(8,128)S(1)} %pad_maximum_fusion.9), channel_id=1, replica_groups=mesh['leaf'=8,'grid'=4] {'grid'}, dimensions={2}, use_global_device_ids=true | all-gather | bytes 40960 | tf_op jit(solution)/shard_map/all_gather | solution.py:69
  269.3 1.5 collective-permute-start.23
  270.8 2.4 collective-permute-done.23
  274.7 5.2 %all-gather.8 = f32[64,128]{1,0:T(8,128)S(1)} all-gather(f32[16,128]{1,0:T(8,128)S(1)} %pad_maximum_fusion.10), channel_id=10, replica_groups=mesh['leaf'=8,'grid'=4] {'grid'}, dimensions={0}, use_global_device_ids=true | all-gather | bytes 40960 | tf_op jit(solution)/shard_map/all_gather | solution.py:42
  (272 shorter events, 43.6 us)
Async XLA Ops:
  7.2 43.8 %reduce-scatter.4.cloned.1.call-start = ((), (), s32[]{:S(2)}) async-start(), calls=%async_computation.3 | async-start | bytes 40960 | tf_op jit(solution)/shard_map/reduce_scatter | solution.py:65
  25.2 38.8 %copy-start.20 = (f32[128,128]{1,0:T(8,128)S(1)}, f32[128,128]{1,0:T(8,128)}, u32[]{:S(2)}) copy-start(f32[128,128]{1,0:T(8,128)} %param.45) | copy-start | bytes 196612
  25.5 4.0 %collective-permute-start = (f32[2,8,512]{2,1,0:T(8,128)S(1)}, f32[2,8,512]{2,1,0:T(8,128)S(1)}, u32[]{:S(2)}, u32[]{:S(2)}) collective-permute-start(f32[2,8,512]{2,1,0:T(8,128)S(1)} %broadcast_select_fusion.1), channel_id=1, source_target_pairs={{0,4},{4,0},{8,12},{12,8},{16,20},{20,16},{24,28},{28,24},{1,5},{5... | collective-permute-start | bytes 98312 | tf_op jit(solution)/shard_map/ppermute | solution.py:14
  27.1 37.9 %copy-start.53 = (s32[128]{0:T(128)}, s32[128]{0:T(128)S(1)}, u32[]{:S(2)}) copy-start(s32[128]{0:T(128)S(1)} %compare_select_fusion.1) | copy-start | bytes 1540
  30.1 68.3 %reduce-scatter.6.cloned.1.call-start = ((), (), s32[]{:S(2)}) async-start(), calls=%async_computation.4 | async-start | bytes 40960 | tf_op jit(solution)/shard_map/reduce_scatter | solution.py:65
  30.9 36.9 %copy-start.37 = (f32[128]{0:T(128)}, f32[128]{0:T(128)S(1)}, u32[]{:S(2)}) copy-start(f32[128]{0:T(128)S(1)} %compare_convert_fusion.4) | copy-start | bytes 1540
  58.8 4.6 %collective-permute-start.1 = (f32[144,128]{1,0:T(8,128)S(1)}, f32[144,128]{1,0:T(8,128)S(1)}, u32[]{:S(2)}, u32[]{:S(2)}) collective-permute-start(f32[144,128]{1,0:T(8,128)S(1)} %reduce_sum.73), channel_id=1, source_target_pairs={{0,4},{4,0},{8,12},{12,8},{16,20},{20,16},{24,28},{28,24},{1,5},{5... | collective-permute-start | bytes 221192 | tf_op jit(solution)/shard_map/ppermute | solution.py:14
  67.7 30.7 %copy-start.24 = (f32[128,128]{1,0:T(8,128)S(1)}, f32[128,128]{1,0:T(8,128)}, u32[]{:S(2)}) copy-start(f32[128,128]{1,0:T(8,128)} %param.49) | copy-start | bytes 196612
  67.7 30.7 %copy-start.30 = (f32[8,128]{1,0:T(8,128)S(1)}, f32[8,128]{1,0:T(8,128)}, u32[]{:S(2)}) copy-start(f32[8,128]{1,0:T(8,128)} %param.48) | copy-start | bytes 12292
  67.8 32.5 %copy-start.22 = (f32[128,128]{1,0:T(8,128)S(1)}, f32[128,128]{1,0:T(8,128)}, u32[]{:S(2)}) copy-start(f32[128,128]{1,0:T(8,128)} %fusion.49) | copy-start | bytes 196612
  67.8 48.1 %copy-start.18 = (f32[128,128]{1,0:T(8,128)S(1)}, f32[128,128]{1,0:T(8,128)}, u32[]{:S(2)}) copy-start(f32[128,128]{1,0:T(8,128)} %param.53) | copy-start | bytes 196612
  69.7 4.3 %collective-permute-start.2 = (f32[2,8,1024]{2,1,0:T(8,128)S(1)}, f32[2,8,1024]{2,1,0:T(8,128)S(1)}, u32[]{:S(2)}, u32[]{:S(2)}) collective-permute-start(f32[2,8,1024]{2,1,0:T(8,128)S(1)} %broadcast_select_fusion), channel_id=1, source_target_pairs={{0,8},{4,12},{8,0},{12,4},{16,24},{20,28},{24,16},{28,20},{1,9},{5... | collective-permute-start | bytes 196616 | tf_op jit(solution)/shard_map/ppermute | solution.py:14
  71.3 47.1 %copy-start.55 = (s32[128]{0:T(128)}, s32[128]{0:T(128)S(1)}, u32[]{:S(2)}) copy-start(s32[128]{0:T(128)S(1)} %compare_select_fusion.2) | copy-start | bytes 1540
  74.1 4.0 %collective-permute-start.3 = (f32[2,8,512]{2,1,0:T(8,128)S(1)}, f32[2,8,512]{2,1,0:T(8,128)S(1)}, u32[]{:S(2)}, u32[]{:S(2)}) collective-permute-start(f32[2,8,512]{2,1,0:T(8,128)S(1)} %slice_select_fusion.3), channel_id=1, source_target_pairs={{0,4},{4,0},{8,12},{12,8},{16,20},{20,16},{24,28},{28,24},{1,5},{5... | collective-permute-start | bytes 98312 | tf_op jit(solution)/shard_map/ppermute | solution.py:14
  78.7 87.1 %reduce-scatter.8.cloned.1.call-start = ((), (), s32[]{:S(2)}) async-start(), calls=%async_computation.5 | async-start | bytes 327680 | tf_op jit(solution)/shard_map/reduce_scatter | solution.py:65
  106.2 4.6 %collective-permute-start.4 = (f32[144,128]{1,0:T(8,128)S(1)}, f32[144,128]{1,0:T(8,128)S(1)}, u32[]{:S(2)}, u32[]{:S(2)}) collective-permute-start(f32[144,128]{1,0:T(8,128)S(1)} %reduce_sum.74), channel_id=1, source_target_pairs={{0,4},{4,0},{8,12},{12,8},{16,20},{20,16},{24,28},{28,24},{1,5},{5... | collective-permute-start | bytes 221192 | tf_op jit(solution)/shard_map/ppermute | solution.py:14
  110.8 4.4 %collective-permute-start.5 = (f32[144,128]{1,0:T(8,128)S(1)}, f32[144,128]{1,0:T(8,128)S(1)}, u32[]{:S(2)}, u32[]{:S(2)}) collective-permute-start(f32[144,128]{1,0:T(8,128)S(1)} %add.191), channel_id=1, source_target_pairs={{0,8},{4,12},{8,0},{12,4},{16,24},{20,28},{24,16},{28,20},{1,9},{5... | collective-permute-start | bytes 221192 | tf_op jit(solution)/shard_map/ppermute | solution.py:14
  119.4 5.5 %collective-permute-start.6 = (f32[1,8,2048]{2,1,0:T(8,128)}, f32[1,8,2048]{2,1,0:T(8,128)}, u32[]{:S(2)}, u32[]{:S(2)}) collective-permute-start(f32[1,8,2048]{2,1,0:T(8,128)} %copy.65), channel_id=1, source_target_pairs={{0,16},{4,20},{8,24},{12,28},{16,0},{20,4},{24,8},{28,12},{1,17},{... | collective-permute-start | bytes 196616 | tf_op jit(solution)/shard_map/ppermute | solution.py:14
  126.4 11.1 %collective-permute-start.7 = (f32[1,8,1024]{1,2,0:T(8,128)S(1)}, f32[1,8,1024]{1,2,0:T(8,128)S(1)}, u32[]{:S(2)}, u32[]{:S(2)}) collective-permute-start(f32[1,8,1024]{1,2,0:T(8,128)S(1)} %slice_select_fusion.1), channel_id=1, source_target_pairs={{0,8},{4,12},{8,0},{12,4},{16,24},{20,28},{24,16},{28,20},{1,9},{5... | collective-permute-start | bytes 98312 | tf_op jit(solution)/shard_map/ppermute | solution.py:14
  128.8 37.0 %copy-start.17 = (f32[128,128]{1,0:T(8,128)S(1)}, f32[128,128]{1,0:T(8,128)}, u32[]{:S(2)}) copy-start(f32[128,128]{1,0:T(8,128)} %param.57) | copy-start | bytes 196612
  128.8 38.0 %copy-start.16 = (f32[128,256]{1,0:T(8,128)S(1)}, f32[128,256]{1,0:T(8,128)}, u32[]{:S(2)}) copy-start(f32[128,256]{1,0:T(8,128)} %param.59) | copy-start | bytes 393220
  128.9 39.3 %copy-start.23 = (f32[128,128]{1,0:T(8,128)S(1)}, f32[128,128]{1,0:T(8,128)}, u32[]{:S(2)}) copy-start(f32[128,128]{1,0:T(8,128)} %fusion.32) | copy-start | bytes 196612
  137.5 38.2 %copy-start.60 = (s32[128]{0:T(128)S(1)}, s32[128]{0:T(128)}, u32[]{:S(2)}) copy-start(s32[128]{0:T(128)} %param.55) | copy-start | bytes 1540
  137.5 42.8 %copy-start.62 = (s32[128]{0:T(128)S(1)}, s32[128]{0:T(128)}, u32[]{:S(2)}) copy-start(s32[128]{0:T(128)} %param.47) | copy-start | bytes 1540
  137.6 48.2 %copy-start.63 = (s32[1,2]{1,0:T(1,128)S(1)}, s32[1,2]{1,0:T(1,128)}, u32[]{:S(2)}) copy-start(s32[1,2]{1,0:T(1,128)} %param.61) | copy-start | bytes 28
  137.6 51.0 %copy-start.11 = (f32[128,128]{1,0:T(8,128)S(1)}, f32[128,128]{1,0:T(8,128)}, u32[]{:S(2)}) copy-start(f32[128,128]{1,0:T(8,128)} %param.58) | copy-start | bytes 196612
  137.6 51.0 %copy-start.57 = (f32[128]{0:T(128)S(1)}, f32[128]{0:T(128)}, u32[]{:S(2)}) copy-start(f32[128]{0:T(128)} %param.60) | copy-start | bytes 1540
  137.6 58.0 %copy-start.56 = (s32[128]{0:T(128)S(1)}, s32[128]{0:T(128)}, u32[]{:S(2)}) copy-start(s32[128]{0:T(128)} %copy-done.55) | copy-start | bytes 1540
  137.6 61.6 %copy-start.7 = (f32[144,128]{1,0:T(8,128)S(1)}, f32[144,128]{1,0:T(8,128)}, u32[]{:S(2)}) copy-start(f32[144,128]{1,0:T(8,128)} %copy-done.6) | copy-start | bytes 221188
  137.6 61.6 %copy-start.13 = (f32[128,128]{1,0:T(8,128)S(1)}, f32[128,128]{1,0:T(8,128)}, u32[]{:S(2)}) copy-start(f32[128,128]{1,0:T(8,128)} %param.50) | copy-start | bytes 196612
  137.6 61.6 %copy-start.42 = (f32[128]{0:T(128)S(1)}, f32[128]{0:T(128)}, u32[]{:S(2)}) copy-start(f32[128]{0:T(128)} %copy-done.41) | copy-start | bytes 1540
  137.6 61.6 %copy-start.51 = (f32[128]{0:T(128)S(1)}, f32[128]{0:T(128)}, u32[]{:S(2)}) copy-start(f32[128]{0:T(128)} %param.52) | copy-start | bytes 1540
  137.7 6.4 %collective-permute-start.8 = (f32[1,8,512]{1,2,0:T(8,128)S(1)}, f32[1,8,512]{1,2,0:T(8,128)S(1)}, u32[]{:S(2)}, u32[]{:S(2)}) collective-permute-start(f32[1,8,512]{1,2,0:T(8,128)S(1)} %slice_select_fusion.2), channel_id=1, source_target_pairs={{0,4},{4,0},{8,12},{12,8},{16,20},{20,16},{24,28},{28,24},{1,5},{5... | collective-permute-start | bytes 49160 | tf_op jit(solution)/shard_map/ppermute | solution.py:14
  174.1 51.6 %copy-start.19 = (f32[128,128]{1,0:T(8,128)S(1)}, f32[128,128]{1,0:T(8,128)}, u32[]{:S(2)}) copy-start(f32[128,128]{1,0:T(8,128)} %param.53) | copy-start | bytes 196612
  174.1 58.5 %copy-start.54 = (s32[128]{0:T(128)S(1)}, s32[128]{0:T(128)}, u32[]{:S(2)}) copy-start(s32[128]{0:T(128)} %copy-done.53) | copy-start | bytes 1540
  174.1 4.6 %collective-permute-start.9 = (f32[144,128]{1,0:T(8,128)S(1)}, f32[144,128]{1,0:T(8,128)S(1)}, u32[]{:S(2)}, u32[]{:S(2)}) collective-permute-start(f32[144,128]{1,0:T(8,128)S(1)} %reduce_sum.75), channel_id=1, source_target_pairs={{0,4},{4,0},{8,12},{12,8},{16,20},{20,16},{24,28},{28,24},{1,5},{5... | collective-permute-start | bytes 221192 | tf_op jit(solution)/shard_map/ppermute | solution.py:14
  175.7 62.7 %copy-start.44 = (f32[128]{0:T(128)S(1)}, f32[128]{0:T(128)}, u32[]{:S(2)}) copy-start(f32[128]{0:T(128)} %copy-done.43) | copy-start | bytes 1540
  178.7 60.1 %copy-start.25 = (f32[128,128]{1,0:T(8,128)S(1)}, f32[128,128]{1,0:T(8,128)}, u32[]{:S(2)}) copy-start(f32[128,128]{1,0:T(8,128)} %param.49) | copy-start | bytes 196612
  178.7 4.4 %collective-permute-start.10 = (f32[144,128]{1,0:T(8,128)S(1)}, f32[144,128]{1,0:T(8,128)S(1)}, u32[]{:S(2)}, u32[]{:S(2)}) collective-permute-start(f32[144,128]{1,0:T(8,128)S(1)} %add.203), channel_id=1, source_target_pairs={{0,8},{4,12},{8,0},{12,4},{16,24},{20,28},{24,16},{28,20},{1,9},{5... | collective-permute-start | bytes 221192 | tf_op jit(solution)/shard_map/ppermute | solution.py:14
  183.2 62.8 %copy-start.5 = (f32[144,128]{1,0:T(8,128)S(1)}, f32[144,128]{1,0:T(8,128)}, u32[]{:S(2)}) copy-start(f32[144,128]{1,0:T(8,128)} %copy-done.4) | copy-start | bytes 221188
  183.2 62.8 %copy-start.15 = (f32[128,128]{1,0:T(8,128)S(1)}, f32[128,128]{1,0:T(8,128)}, u32[]{:S(2)}) copy-start(f32[128,128]{1,0:T(8,128)} %param.42) | copy-start | bytes 196612
  183.2 62.8 %copy-start.38 = (f32[128]{0:T(128)S(1)}, f32[128]{0:T(128)}, u32[]{:S(2)}) copy-start(f32[128]{0:T(128)} %copy-done.37) | copy-start | bytes 1540
  183.2 62.8 %copy-start.52 = (f32[128]{0:T(128)S(1)}, f32[128]{0:T(128)}, u32[]{:S(2)}) copy-start(f32[128]{0:T(128)} %param.44) | copy-start | bytes 1540
  183.2 5.3 %collective-permute-start.11 = (f32[144,128]{1,0:T(8,128)S(1)}, f32[144,128]{1,0:T(8,128)S(1)}, u32[]{:S(2)}, u32[]{:S(2)}) collective-permute-start(f32[144,128]{1,0:T(8,128)S(1)} %add.204), channel_id=1, source_target_pairs={{0,16},{4,20},{8,24},{12,28},{16,0},{20,4},{24,8},{28,12},{1,17},{... | collective-permute-start | bytes 221192 | tf_op jit(solution)/shard_map/ppermute | solution.py:14
  194.1 3.6 %collective-permute-start.12 = (f32[8,128]{1,0:T(8,128)S(1)}, f32[8,128]{1,0:T(8,128)S(1)}, u32[]{:S(2)}, u32[]{:S(2)}) collective-permute-start(f32[8,128]{1,0:T(8,128)S(1)} %bitcast_reduce_fusion), channel_id=1, source_target_pairs={{0,4},{4,0},{8,12},{12,8},{16,20},{20,16},{24,28},{28,24},{1,5},{5... | collective-permute-start | bytes 12296 | tf_op jit(solution)/shard_map/ppermute | solution.py:14
  197.7 3.6 %collective-permute-start.13 = (f32[8,128]{1,0:T(8,128)S(1)}, f32[8,128]{1,0:T(8,128)S(1)}, u32[]{:S(2)}, u32[]{:S(2)}) collective-permute-start(f32[8,128]{1,0:T(8,128)S(1)} %add.207), channel_id=1, source_target_pairs={{0,8},{4,12},{8,0},{12,4},{16,24},{20,28},{24,16},{28,20},{1,9},{5... | collective-permute-start | bytes 12296 | tf_op jit(solution)/shard_map/ppermute | solution.py:14
  201.4 4.5 %collective-permute-start.14 = (f32[8,128]{1,0:T(8,128)S(1)}, f32[8,128]{1,0:T(8,128)S(1)}, u32[]{:S(2)}, u32[]{:S(2)}) collective-permute-start(f32[8,128]{1,0:T(8,128)S(1)} %add.208), channel_id=1, source_target_pairs={{0,16},{4,20},{8,24},{12,28},{16,0},{20,4},{24,8},{28,12},{1,17},{... | collective-permute-start | bytes 12296 | tf_op jit(solution)/shard_map/ppermute | solution.py:14
  206.0 46.7 %copy-start.31 = (f32[8,128]{1,0:T(8,128)}, f32[8,128]{1,0:T(8,128)S(1)}, u32[]{:S(2)}) copy-start(f32[8,128]{1,0:T(8,128)S(1)} %convolution_add_fusion.3) | copy-start | bytes 12292
  211.5 3.7 %collective-permute-start.15 = (f32[1,8,512]{2,1,0:T(8,128)S(1)}, f32[1,8,512]{2,1,0:T(8,128)S(1)}, u32[]{:S(2)}, u32[]{:S(2)}) collective-permute-start(f32[1,8,512]{2,1,0:T(8,128)S(1)} %bitcast.142), channel_id=1, source_target_pairs={{0,4},{4,0},{8,12},{12,8},{16,20},{20,16},{24,28},{28,24},{1,5},{5... | collective-permute-start | bytes 49160 | tf_op jit(solution)/shard_map/ppermute | solution.py:14
  215.2 3.9 %collective-permute-start.16 = (f32[1,8,1024]{2,1,0:T(8,128)S(1)}, f32[1,8,1024]{2,1,0:T(8,128)S(1)}, u32[]{:S(2)}, u32[]{:S(2)}) collective-permute-start(f32[1,8,1024]{2,1,0:T(8,128)S(1)} %maximum_select_fusion.6), channel_id=1, source_target_pairs={{0,8},{4,12},{8,0},{12,4},{16,24},{20,28},{24,16},{28,20},{1,9},{5... | collective-permute-start | bytes 98312 | tf_op jit(solution)/shard_map/ppermute | solution.py:14
  219.1 5.2 %collective-permute-start.17 = (f32[1,8,2048]{2,1,0:T(8,128)S(1)}, f32[1,8,2048]{2,1,0:T(8,128)S(1)}, u32[]{:S(2)}, u32[]{:S(2)}) collective-permute-start(f32[1,8,2048]{2,1,0:T(8,128)S(1)} %maximum_select_fusion.2), channel_id=1, source_target_pairs={{0,16},{4,20},{8,24},{12,28},{16,0},{20,4},{24,8},{28,12},{1,17},{... | collective-permute-start | bytes 196616 | tf_op jit(solution)/shard_map/ppermute | solution.py:14
  225.0 29.2 %copy-start.21 = (f32[128,128]{1,0:T(8,128)S(1)}, f32[128,128]{1,0:T(8,128)}, u32[]{:S(2)}) copy-start(f32[128,128]{1,0:T(8,128)} %param.45) | copy-start | bytes 196612
  225.0 38.2 %copy-start.40 = (f32[128]{0:T(128)S(1)}, f32[128]{0:T(128)}, u32[]{:S(2)}) copy-start(f32[128]{0:T(128)} %copy-done.39) | copy-start | bytes 1540
  225.0 38.6 %copy-start.27 = (f32[128,128]{1,0:T(8,128)S(1)}, f32[128,128]{1,0:T(8,128)}, u32[]{:S(2)}) copy-start(f32[128,128]{1,0:T(8,128)} %param.41) | copy-start | bytes 196612
  225.0 45.7 %copy-start.47 = (s32[256]{0:T(256)S(1)}, s32[256]{0:T(256)}, u32[]{:S(2)}) copy-start(s32[256]{0:T(256)} %copy-done.46) | copy-start | bytes 3076
  231.1 3.7 %collective-permute-start.18 = (f32[16,128]{1,0:T(8,128)S(1)}, f32[16,128]{1,0:T(8,128)S(1)}, u32[]{:S(2)}, u32[]{:S(2)}) collective-permute-start(f32[16,128]{1,0:T(8,128)S(1)} %reduce_sum.77), channel_id=1, source_target_pairs={{0,4},{4,0},{8,12},{12,8},{16,20},{20,16},{24,28},{28,24},{1,5},{5... | collective-permute-start | bytes 24584 | tf_op jit(solution)/shard_map/ppermute | solution.py:14
  234.8 3.7 %collective-permute-start.19 = (f32[16,128]{1,0:T(8,128)S(1)}, f32[16,128]{1,0:T(8,128)S(1)}, u32[]{:S(2)}, u32[]{:S(2)}) collective-permute-start(f32[16,128]{1,0:T(8,128)S(1)} %add.211), channel_id=1, source_target_pairs={{0,8},{4,12},{8,0},{12,4},{16,24},{20,28},{24,16},{28,20},{1,9},{5... | collective-permute-start | bytes 24584 | tf_op jit(solution)/shard_map/ppermute | solution.py:14
  239.3 34.3 %copy-start.32 = (f32[8,128]{1,0:T(8,128)}, f32[8,128]{1,0:T(8,128)S(1)}, u32[]{:S(2)}) copy-start(f32[8,128]{1,0:T(8,128)S(1)} %convolution_add_fusion.2) | copy-start | bytes 12292
  244.5 3.9 %collective-permute-start.20 = (f32[2,8,512]{2,1,0:T(8,128)S(1)}, f32[2,8,512]{2,1,0:T(8,128)S(1)}, u32[]{:S(2)}, u32[]{:S(2)}) collective-permute-start(f32[2,8,512]{2,1,0:T(8,128)S(1)} %all_gather.70), channel_id=1, source_target_pairs={{0,4},{4,0},{8,12},{12,8},{16,20},{20,16},{24,28},{28,24},{1,5},{5... | collective-permute-start | bytes 98312 | tf_op jit(solution)/shard_map/ppermute | solution.py:14
  248.4 4.3 %collective-permute-start.21 = (f32[2,8,1024]{2,1,0:T(8,128)S(1)}, f32[2,8,1024]{2,1,0:T(8,128)S(1)}, u32[]{:S(2)}, u32[]{:S(2)}) collective-permute-start(f32[2,8,1024]{2,1,0:T(8,128)S(1)} %maximum_select_fusion.4), channel_id=1, source_target_pairs={{0,8},{4,12},{8,0},{12,4},{16,24},{20,28},{24,16},{28,20},{1,9},{5... | collective-permute-start | bytes 196616 | tf_op jit(solution)/shard_map/ppermute | solution.py:14
  252.8 27.3 %copy-start.3 = (f32[128,256]{1,0:T(8,128)S(1)}, f32[128,256]{1,0:T(8,128)}, u32[]{:S(2)}) copy-start(f32[128,256]{1,0:T(8,128)} %param.35) | copy-start | bytes 393220
  252.8 27.5 %copy-start.28 = (f32[128,128]{1,0:T(8,128)S(1)}, f32[128,128]{1,0:T(8,128)}, u32[]{:S(2)}) copy-start(f32[128,128]{1,0:T(8,128)} %param.33) | copy-start | bytes 196612
  259.5 3.7 %collective-permute-start.22 = (f32[16,128]{1,0:T(8,128)S(1)}, f32[16,128]{1,0:T(8,128)S(1)}, u32[]{:S(2)}, u32[]{:S(2)}) collective-permute-start(f32[16,128]{1,0:T(8,128)S(1)} %reduce_sum.78), channel_id=1, source_target_pairs={{0,4},{4,0},{8,12},{12,8},{16,20},{20,16},{24,28},{28,24},{1,5},{5... | collective-permute-start | bytes 24584 | tf_op jit(solution)/shard_map/ppermute | solution.py:14
  269.3 3.9 %collective-permute-start.23 = (f32[2,8,512]{2,1,0:T(8,128)S(1)}, f32[2,8,512]{2,1,0:T(8,128)S(1)}, u32[]{:S(2)}, u32[]{:S(2)}) collective-permute-start(f32[2,8,512]{2,1,0:T(8,128)S(1)} %all_gather.73), channel_id=1, source_target_pairs={{0,4},{4,0},{8,12},{12,8},{16,20},{20,16},{24,28},{28,24},{1,5},{5... | collective-permute-start | bytes 98312 | tf_op jit(solution)/shard_map/ppermute | solution.py:14
  (27 other events, 231.7 us)
Sparse Core Ops, SparseCore 0:
  30.3 20.6 reduce-scatter.3
  78.8 19.5 reduce-scatter.5
  145.0 20.7 reduce-scatter.7
